TPU v7x, 32 devices: a whole 2x2x4 slice. The times are simulated.
32 devices in a mesh: wide: 8 (over z, core), narrow: 4 (over y, x).
Axes of the slice: x: 2, y: 2, z: 4, core: 2. Of those that a mesh axis runs over, the one named last changes fastest.
Arguments:
- pixel_stack: float32 [128, 64, 2048], P(('wide', 'narrow')), may hold values from -6 to 6
- quality_weight: float32 [128, 64, 2048], P(('wide', 'narrow')), may hold values from 0.2 to 1
Outputs:
- slope: float32 [64, 2048], P('wide', 'narrow')
- level: float32 [64, 2048], P('wide', 'narrow')
- anomaly: bfloat16 [128, 64, 2048], P(None, 'wide', 'narrow')
All inputs are finite; a program needn't handle non-finite values.
Results may differ from a plain program's by a relative error of at most 0.001.
Values sent between devices are 32-bit elements; how exact they have to be, the bound alone decides.
No kernel may reach another device: no remote copies, remote signals or barrier semaphores. Data moves between devices by JAX's collectives and lax.ppermute only.
A program may use at most 64 MiB of HBM per device.

v0:
```python
import jax
import jax.numpy as jnp
from jax import lax
from jax.sharding import PartitionSpec as P


def fit_trend(series, weight_series, axis):
    count = series.shape[axis]
    shape = [1] * series.ndim
    shape[axis] = count
    centred = ((jnp.arange(count).astype(jnp.float32) - (count - 1) / 2.0) / count).reshape(shape)
    weighted = weight_series * series
    first = jnp.sum(weight_series, axis=axis, keepdims=True)
    second = jnp.sum(weight_series * centred, axis=axis, keepdims=True)
    third = jnp.sum(weight_series * centred * centred, axis=axis, keepdims=True)
    plain_sum = jnp.sum(weighted, axis=axis, keepdims=True)
    moment_sum = jnp.sum(weighted * centred, axis=axis, keepdims=True)
    determinant = first * third - second * second
    slope = (first * moment_sum - second * plain_sum) / determinant
    level = (third * plain_sum - second * moment_sum) / determinant
    anomaly = (series - level - slope * centred).astype(jnp.bfloat16)
    return (slope, level, anomaly)


def body(pixel_stack, quality_weight):
    wide_count = lax.axis_size("wide")
    narrow_count = lax.axis_size("narrow")
    local_steps = pixel_stack.shape[0]
    rows_tile = pixel_stack.shape[1] // wide_count
    cols_tile = pixel_stack.shape[2] // narrow_count

    def tile_major(field):
        split = field.reshape(local_steps, wide_count, rows_tile, narrow_count, cols_tile)
        return split.transpose(1, 3, 0, 2, 4).reshape(
            wide_count * narrow_count, local_steps, rows_tile, cols_tile
        )

    slope, level, anomaly = fit_trend(
        lax.all_to_all(
            tile_major(pixel_stack), ("wide", "narrow"), split_axis=0, concat_axis=1, tiled=True
        ),
        lax.all_to_all(
            tile_major(quality_weight), ("wide", "narrow"), split_axis=0, concat_axis=1, tiled=True
        ),
        1,
    )
    return (
        slope.reshape(rows_tile, cols_tile),
        level.reshape(rows_tile, cols_tile),
        anomaly.reshape(-1, rows_tile, cols_tile),
    )


def solution(mesh):
    return jax.shard_map(
        body,
        mesh=mesh,
        in_specs=(P(("wide", "narrow"), None, None), P(("wide", "narrow"), None, None)),
        out_specs=(P("wide", "narrow"), P("wide", "narrow"), P(None, "wide", "narrow")),
        check_vma=False,
    )
```

profile of v0, /device:TPU:0, one launch (start us, length us, event | category | flops | bytes accessed | tf_op | source)
XLA Modules:
  0.0 116.6 jit_solution(14845793955616364501)
XLA Ops:
  0.6 3.1 %copy.6 = f32[8,4,4,8,512]{4,3,2,1,0:T(8,128)} copy(f32[8,4,4,8,512]{4,3,1,0,2:T(8,128)} %bitcast.16) | data formatting | bytes 4194304 | tf_op jit(solution)/shard_map/transpose | solution.py:34
  3.8 7.3 %all-to-all-start.1 = ((f32[32,4,8,512]{3,2,1,0:T(8,128)}), f32[32,4,8,512]{3,2,1,0:T(8,128)S(1)}, u32[]{:S(2)}, u32[]{:S(2)}) async-start(f32[32,4,8,512]{3,2,1,0:T(8,128)} %bitcast.15), calls=%async_computation.1 | async-start | bytes 4194304 | tf_op jit(solution)/shard_map/all_to_all | solution.py:39
  11.1 3.2 %copy.5 = f32[8,4,4,8,512]{4,3,2,1,0:T(8,128)} copy(f32[8,4,4,8,512]{4,3,1,0,2:T(8,128)} %bitcast.17) | data formatting | bytes 4194304 | tf_op jit(solution)/shard_map/transpose | solution.py:34
  14.3 45.5 %all-to-all-done.1 = f32[32,4,8,512]{3,2,1,0:T(8,128)S(1)} async-done(((f32[32,4,8,512]{3,2,1,0:T(8,128)}), f32[32,4,8,512]{3,2,1,0:T(8,128)S(1)}, u32[]{:S(2)}, u32[]{:S(2)}) %all-to-all-start.1) | async-done | bytes 2097184 | tf_op jit(solution)/shard_map/all_to_all | solution.py:39
  59.8 4.5 %all-to-all-start = ((f32[32,4,8,512]{3,2,1,0:T(8,128)}), f32[32,4,8,512]{3,2,1,0:T(8,128)}, u32[]{:S(2)}, u32[]{:S(2)}) async-start(f32[32,4,8,512]{3,2,1,0:T(8,128)} %bitcast.14), calls=%async_computation | async-start | bytes 4194304 | tf_op jit(solution)/shard_map/all_to_all | solution.py:42
  64.4 48.6 %all-to-all-done = f32[32,4,8,512]{3,2,1,0:T(8,128)} async-done(((f32[32,4,8,512]{3,2,1,0:T(8,128)}), f32[32,4,8,512]{3,2,1,0:T(8,128)}, u32[]{:S(2)}, u32[]{:S(2)}) %all-to-all-start) | async-done | bytes 2097184 | tf_op jit(solution)/shard_map/all_to_all | solution.py:42
  113.0 2.2 %multiply_reduce_fusion = (f32[8,512]{1,0:T(8,128)S(1)}, f32[8,512]{1,0:T(8,128)S(1)}, f32[8,512]{1,0:T(8,128)S(1)}, f32[8,512]{1,0:T(8,128)S(1)}, f32[8,512]{1,0:T(8,128)S(1)}) fusion(f32[32,4,8,512]{3,2,1,0:T(8,128)} %all-to-all-done, f32[32,4]{1,0:T(8,128)S(1)} %add_multiply_fusion, f32[32,4,8,512]{3,2,1,0:T(8,128)S(1)} %all-to-all-done.1), kind=kLoop, calls=%fused_computation.3 | loop fusion | flops 4698112 | bytes 4276736 | tf_op jit(solution)/shard_map/reduce_sum | solution.py:15
  115.2 0.0 copy-start
  115.3 0.0 copy-start.1
  115.3 1.3 %fusion.1 = bf16[128,8,512]{2,1,0:T(8,128)(2,1)} fusion(f32[32,4,8,512]{3,2,1,0:T(8,128)S(1)} %all-to-all-done.1, f32[128]{0:T(128)S(1)} %add_multiply_fusion.1, f32[8,512]{1,0:T(8,128)S(1)} %get-tuple-element.11, f32[8,512]{1,0:T(8,128)S(1)} %get-tuple-element.10), kind=kLoop, calls=%fused_computation.2 | loop fusion | flops 2097152 | bytes 3179008 | tf_op jit(solution)/shard_map/convert_element_type | solution.py:21
  116.6 0.0 copy-done
  116.6 0.0 copy-done.1
  (3 shorter events, 0.0 us)
Async XLA Ops:
  3.8 56.0 %all-to-all-start.1 = ((f32[32,4,8,512]{3,2,1,0:T(8,128)}), f32[32,4,8,512]{3,2,1,0:T(8,128)S(1)}, u32[]{:S(2)}, u32[]{:S(2)}) async-start(f32[32,4,8,512]{3,2,1,0:T(8,128)} %bitcast.15), calls=%async_computation.1 | async-start | bytes 4194304 | tf_op jit(solution)/shard_map/all_to_all | solution.py:39
  59.8 53.2 %all-to-all-start = ((f32[32,4,8,512]{3,2,1,0:T(8,128)}), f32[32,4,8,512]{3,2,1,0:T(8,128)}, u32[]{:S(2)}, u32[]{:S(2)}) async-start(f32[32,4,8,512]{3,2,1,0:T(8,128)} %bitcast.14), calls=%async_computation | async-start | bytes 4194304 | tf_op jit(solution)/shard_map/all_to_all | solution.py:42
  115.2 1.3 %copy-start = (f32[8,512]{1,0:T(8,128)}, f32[8,512]{1,0:T(8,128)S(1)}, u32[]{:S(2)}) copy-start(f32[8,512]{1,0:T(8,128)S(1)} %get-tuple-element.10) | copy-start | bytes 49156
  115.3 1.3 %copy-start.1 = (f32[8,512]{1,0:T(8,128)}, f32[8,512]{1,0:T(8,128)S(1)}, u32[]{:S(2)}) copy-start(f32[8,512]{1,0:T(8,128)S(1)} %get-tuple-element.11) | copy-start | bytes 49156
where the time goes:
time: 117 us
  waiting for transfers between devices  94.1 us (80%)
  starting transfers between devices  11.9 us (10%)
  local copies, waits for them, and re-layouts  6.34 us (5%)
  other arithmetic  3.55 us (3%)
    all_to_all x1, waiting for transfers between devices, body(): lax.all_to_all(tile_major(quality_weight), ('wide', 'narrow'), split_axis...  48.6 us
    all_to_all x1, waiting for transfers between devices, body(): lax.all_to_all(tile_major(pixel_stack), ('wide', 'narrow'), split_axis=0,...  45.5 us
    all_to_all x1, starting transfers between devices, body(): lax.all_to_all(tile_major(pixel_stack), ('wide', 'narrow'), split_axis=0,...  7.33 us
    transpose x2, local copies, waits for them, and re-layouts, tile_major(): split.transpose(1, 3, 0, 2, 4)  6.32 us
    all_to_all x1, starting transfers between devices, body(): lax.all_to_all(tile_major(quality_weight), ('wide', 'narrow'), split_axis...  4.55 us
  transfers between devices with their start and end apart: 2, of which 2 were waited for; matrix products, arithmetic and copies ran while one was open for 3% of the time, Pallas kernels for 0%

commit v1 on v0

v1 whole, which is shorter than its diff:
```python
import jax
import jax.numpy as jnp
from jax import lax
from jax.sharding import PartitionSpec as P


def body(pixel_stack, quality_weight):
    wide_count = lax.axis_size("wide")
    narrow_count = lax.axis_size("narrow")
    wide = lax.axis_index("wide")
    narrow = lax.axis_index("narrow")
    local_steps = pixel_stack.shape[0]
    rows_tile = pixel_stack.shape[1] // wide_count
    cols_tile = pixel_stack.shape[2] // narrow_count
    count = local_steps * wide_count * narrow_count

    split = pixel_stack.reshape(local_steps, wide_count, rows_tile, narrow_count, cols_tile)
    tiles = split.transpose(1, 3, 0, 2, 4).reshape(
        wide_count * narrow_count, local_steps, rows_tile, cols_tile
    )
    series = lax.all_to_all(tiles, ("wide", "narrow"), split_axis=0, concat_axis=1, tiled=True)
    series = series.reshape(count, rows_tile, cols_tile)

    first_step = (wide * narrow_count + narrow) * local_steps
    steps = (first_step + jnp.arange(local_steps)).astype(jnp.float32)
    centred = ((steps - (count - 1) / 2.0) / count).reshape(local_steps, 1, 1)
    weighted = quality_weight * pixel_stack
    sums = jnp.stack([
        jnp.sum(quality_weight, axis=0),
        jnp.sum(quality_weight * centred, axis=0),
        jnp.sum(quality_weight * centred * centred, axis=0),
        jnp.sum(weighted, axis=0),
        jnp.sum(weighted * centred, axis=0),
    ])
    sums = sums.reshape(5, wide_count, rows_tile, narrow_count, cols_tile).transpose(1, 3, 0, 2, 4)

    def halve(sums, axis, bit):
        dim = 0 if axis == "wide" else 1
        size = lax.axis_size(axis)
        index = lax.axis_index(axis)
        return None

    def exchange(part, axis, bit):
        size = lax.axis_size(axis)
        return lax.ppermute(part, axis, [(i, i ^ bit) for i in range(size)])

    shape = sums.shape
    half = wide_count // 2
    s = sums.reshape(half, 2, narrow_count, 5, rows_tile, cols_tile)
    mine = wide % 2
    keep = lax.dynamic_index_in_dim(s, mine, 1, keepdims=False)
    send = lax.dynamic_index_in_dim(s, 1 - mine, 1, keepdims=False)
    s = keep + exchange(send, "wide", 1)
    total = lax.dynamic_index_in_dim(s, narrow, 1, keepdims=False)
    for d in range(1, narrow_count):
        part = lax.dynamic_index_in_dim(s, narrow ^ d, 1, keepdims=False)
        total = total + exchange(part, "narrow", d)
    s = total
    bit = 1
    while bit < half:
        n = s.shape[0]
        s = s.reshape(n // 2, 2, 5, rows_tile, cols_tile)
        mine = (wide // (2 * bit)) % 2
        keep = lax.dynamic_index_in_dim(s, mine, 1, keepdims=False)
        send = lax.dynamic_index_in_dim(s, 1 - mine, 1, keepdims=False)
        s = keep + exchange(send, "wide", 2 * bit)
        bit *= 2
    first, second, third, plain_sum, moment_sum = [s[0, i] for i in range(5)]
    determinant = first * third - second * second
    slope = (first * moment_sum - second * plain_sum) / determinant
    level = (third * plain_sum - second * moment_sum) / determinant
    every = ((jnp.arange(count).astype(jnp.float32) - (count - 1) / 2.0) / count).reshape(count, 1, 1)
    anomaly = (series - level[None] - slope[None] * every).astype(jnp.bfloat16)
    return slope, level, anomaly


def solution(mesh):
    return jax.shard_map(
        body,
        mesh=mesh,
        in_specs=(P(("wide", "narrow"), None, None), P(("wide", "narrow"), None, None)),
        out_specs=(P("wide", "narrow"), P("wide", "narrow"), P(None, "wide", "narrow")),
        check_vma=False,
    )
```

time: 117 us -> 70.5 us (0.60)
  waiting for transfers between devices: 94.1 us -> 39.9 us
  other arithmetic: 3.55 us -> 8.62 us
  starting transfers between devices: 11.9 us -> 13.4 us
    all_to_all x2 -> x1, waiting for transfers between devices: 94.1 us -> 0.01 us  [body(): lax.all_to_all(tiles, ('wide', 'narrow'), split_axis=0, concat_axis=1, ti...]
    ppermute x0 -> x6, waiting for transfers between devices: none -> 39.9 us  [exchange(): return lax.ppermute(part, axis, [(i, i ^ bit) for i in range(size)])]
    ppermute x0 -> x6, starting transfers between devices: none -> 5.92 us  [exchange(): return lax.ppermute(part, axis, [(i, i ^ bit) for i in range(size)])]
    all_to_all x2 -> x1, starting transfers between devices: 11.9 us -> 7.45 us  [body(): lax.all_to_all(tiles, ('wide', 'narrow'), split_axis=0, concat_axis=1, ti...]
    transpose x2 -> x1, local copies, waits for them, and re-layouts: 6.32 us -> 3.21 us  [body(): split.transpose(1, 3, 0, 2, 4)]
    unnamed x4 -> x12, local copies, waits for them, and re-layouts: 0.01 us -> 2.63 us
    add x0 -> x4, other arithmetic: none -> 2.13 us  [the longest x1 1.99 us: body(): s = keep + exchange(send, 'wide', 1)]
    convert_element_type x1, other arithmetic: 1.28 us -> 2.86 us  [body(): anomaly = (series - level[None] - slope[None] * every).astype(jnp.bfloat16)]
  transfers between devices with their start and end apart: 2 -> 7, of which waited for: 2 -> 6; matrix products, arithmetic and copies ran while one was open for 3% -> 14% of each run, Pallas kernels for 0% -> 0%
where the time goes in v1:
time: 70.5 us; the launch traced here: 70.1 us
  waiting for transfers between devices  39.9 us (57%)
  starting transfers between devices  13.4 us (19%)
  other arithmetic  8.62 us (12%)
  local copies, waits for them, and re-layouts  7.36 us (10%)
  between operations  0.8 us (1%)
    ppermute x6, waiting for transfers between devices, exchange(): return lax.ppermute(part, axis, [(i, i ^ bit) for i in range(size)])  39.9 us
    all_to_all x1, starting transfers between devices, body(): lax.all_to_all(tiles, ('wide', 'narrow'), split_axis=0, concat_axis=1, ti...  7.45 us
    ppermute x6, starting transfers between devices, exchange(): return lax.ppermute(part, axis, [(i, i ^ bit) for i in range(size)])  5.92 us
    reduce_sum x1, other arithmetic, body(): jnp.sum(weighted * centred, axis=0)  3.59 us
    transpose x1, local copies, waits for them, and re-layouts, body(): split.transpose(1, 3, 0, 2, 4)  3.21 us
    convert_element_type x1, other arithmetic, body(): anomaly = (series - level[None] - slope[None] * every).astype(jnp.bfloat16)  2.86 us
    unnamed x12, local copies, waits for them, and re-layouts  2.63 us
    add x1, other arithmetic, body(): s = keep + exchange(send, 'wide', 1)  1.99 us
  transfers between devices with their start and end apart: 7, of which 6 were waited for; matrix products, arithmetic and copies ran while one was open for 14% of the time, Pallas kernels for 0%

profile of v1, /device:TPU:0, one launch (start us, length us, event | category | flops | bytes accessed | tf_op | source)
XLA Modules:
  0.0 70.1 jit_solution(16543709485021986502)
XLA Ops:
  0.6 3.2 %copy.7 = f32[8,4,4,8,512]{4,3,2,1,0:T(8,128)} copy(f32[8,4,4,8,512]{4,3,1,0,2:T(8,128)} %bitcast.43) | data formatting | bytes 4194304 | tf_op jit(solution)/shard_map/transpose | solution.py:18
  3.8 0.0 copy-start
  3.8 7.5 %all-to-all-start = ((f32[32,4,8,512]{3,2,1,0:T(8,128)}), f32[32,4,8,512]{3,2,1,0:T(8,128)}, u32[]{:S(2)}, u32[]{:S(2)}) async-start(f32[32,4,8,512]{3,2,1,0:T(8,128)} %bitcast.44), calls=%async_computation | async-start | bytes 4194304 | tf_op jit(solution)/shard_map/all_to_all | solution.py:21
  11.3 0.0 copy-done
  11.3 3.6 %multiply_reduce_fusion = (f32[64,2048]{1,0:T(8,128)S(1)}, f32[64,2048]{1,0:T(8,128)}, f32[64,2048]{1,0:T(8,128)}, f32[64,2048]{1,0:T(8,128)S(1)}, f32[64,2048]{1,0:T(8,128)S(1)}) fusion(f32[4]{0:T(128)S(1)} %add_multiply_fusion.1, f32[4,64,2048]{2,1,0:T(8,128)} %param.3, f32[4,64,2048]{2,1,0:T(8,128)S(1)} %copy-done), kind=kLoop, calls=%fused_computation.3 | loop fusion | flops 4063232 | bytes 6815760 | tf_op jit(solution)/shard_map/reduce_sum | solution.py:33
  15.0 1.1 %constant_dynamic-update-slice_fusion.2 = f32[5,8,8,4,512]{4,2,0,3,1:T(8,128)S(1)} fusion(f32[5,8,8,4,512]{4,2,0,3,1:T(8,128)S(1)} %constant_dynamic-update-slice_fusion.3, f32[1,8,8,4,512]{4,2,0,3,1:T(8,128)} %bitcast.49), kind=kLoop, calls=%fused_computation.23 | loop fusion | bytes 1048576
  16.1 1.1 %constant_dynamic-update-slice_fusion.1 = f32[5,8,8,4,512]{4,2,0,3,1:T(8,128)S(1)} fusion(f32[5,8,8,4,512]{4,2,0,3,1:T(8,128)S(1)} %constant_dynamic-update-slice_fusion.2, f32[1,8,8,4,512]{4,2,0,3,1:T(8,128)} %bitcast.48), kind=kLoop, calls=%fused_computation.22 | loop fusion | bytes 1048576
  17.3 0.0 copy-start.1
  17.3 1.4 %dynamic-slice_bitcast_fusion = f32[4,4,5,8,512]{4,3,2,1,0:T(8,128)} fusion(f32[4,2,4,5,8,512]{5,4,3,2,1,0:T(8,128)S(1)} %bitcast.45, s32[]{:T(128)S(6)} %select_n.58), kind=kLoop, calls=%fused_computation.7 | loop fusion | bytes 2621444 | tf_op jit(solution)/shard_map/jit(dynamic_index_in_dim)/squeeze | solution.py:52
  18.6 0.2 collective-permute-start
  18.8 0.4 copy-done.1
  19.2 2.8 %collective-permute-done = f32[4,4,5,8,512]{4,3,2,1,0:T(8,128)} collective-permute-done((f32[4,4,5,8,512]{4,3,2,1,0:T(8,128)}, f32[4,4,5,8,512]{4,3,2,1,0:T(8,128)}, u32[]{:S(2)}, u32[]{:S(2)}) %collective-permute-start) | collective-permute-done | bytes 1310752 | tf_op jit(solution)/shard_map/ppermute | solution.py:45
  22.0 2.0 %bitcast_add_fusion = f32[4,4,5,8,512]{4,3,2,1,0:T(8,128)S(1)} fusion(f32[4,4,5,8,512]{4,3,2,1,0:T(8,128)} %collective-permute-done, f32[4,2,4,5,8,512]{5,4,3,2,1,0:T(8,128)} %bitcast.46, s32[]{:T(128)S(6)} %select_n.57), kind=kLoop, calls=%fused_computation.6 | loop fusion | flops 327680 | bytes 3932164 | tf_op jit(solution)/shard_map/add | solution.py:53
  24.0 0.1 dynamic-slice_bitcast_fusion.3
  24.1 2.7 %collective-permute-start.3 = (f32[4,5,8,512]{3,2,1,0:T(8,128)S(1)}, f32[4,5,8,512]{3,2,1,0:T(8,128)S(1)}, u32[]{:S(2)}, u32[]{:S(2)}) collective-permute-start(f32[4,5,8,512]{3,2,1,0:T(8,128)S(1)} %get-tuple-element.9), channel_id=1, source_target_pairs={{0,3},{1,2},{2,1},{3,0},{4,7},{5,6},{6,5},{7,4},{8,11},{9,10},{10,... | collective-permute-start | bytes 983048 | tf_op jit(solution)/shard_map/ppermute | solution.py:45
  26.8 0.6 collective-permute-start.2
  27.3 0.3 collective-permute-start.1
  27.6 16.7 %collective-permute-done.3 = f32[4,5,8,512]{3,2,1,0:T(8,128)S(1)} collective-permute-done((f32[4,5,8,512]{3,2,1,0:T(8,128)S(1)}, f32[4,5,8,512]{3,2,1,0:T(8,128)S(1)}, u32[]{:S(2)}, u32[]{:S(2)}) %collective-permute-start.3) | collective-permute-done | bytes 327712 | tf_op jit(solution)/shard_map/ppermute | solution.py:45
  44.4 5.2 %collective-permute-done.2 = f32[4,5,8,512]{3,2,1,0:T(8,128)S(1)} collective-permute-done((f32[4,5,8,512]{3,2,1,0:T(8,128)S(1)}, f32[4,5,8,512]{3,2,1,0:T(8,128)S(1)}, u32[]{:S(2)}, u32[]{:S(2)}) %collective-permute-start.2) | collective-permute-done | bytes 327712 | tf_op jit(solution)/shard_map/ppermute | solution.py:45
  49.5 1.9 %collective-permute-done.1 = f32[4,5,8,512]{3,2,1,0:T(8,128)S(1)} collective-permute-done((f32[4,5,8,512]{3,2,1,0:T(8,128)S(1)}, f32[4,5,8,512]{3,2,1,0:T(8,128)S(1)}, u32[]{:S(2)}, u32[]{:S(2)}) %collective-permute-start.1) | collective-permute-done | bytes 327712 | tf_op jit(solution)/shard_map/ppermute | solution.py:45
  51.4 0.1 fusion.3
  51.5 1.7 %collective-permute-start.4 = (f32[2,5,8,512]{3,2,1,0:T(8,128)S(1)}, f32[2,5,8,512]{3,2,1,0:T(8,128)S(1)}, u32[]{:S(2)}, u32[]{:S(2)}) collective-permute-start(f32[2,5,8,512]{3,2,1,0:T(8,128)S(1)} %dynamic-slice_bitcast_fusion.4), channel_id=1, source_target_pairs={{0,8},{4,12},{8,0},{12,4},{16,24},{20,28},{24,16},{28,20},{1,9},{5... | collective-permute-start | bytes 491528 | tf_op jit(solution)/shard_map/ppermute | solution.py:45
  53.3 7.6 %collective-permute-done.4 = f32[2,5,8,512]{3,2,1,0:T(8,128)S(1)} collective-permute-done((f32[2,5,8,512]{3,2,1,0:T(8,128)S(1)}, f32[2,5,8,512]{3,2,1,0:T(8,128)S(1)}, u32[]{:S(2)}, u32[]{:S(2)}) %collective-permute-start.4) | collective-permute-done | bytes 163872 | tf_op jit(solution)/shard_map/ppermute | solution.py:45
  60.9 0.5 collective-permute-start.5
  61.4 5.7 %collective-permute-done.5 = f32[1,5,8,512]{3,2,1,0:T(8,128)S(1)} collective-permute-done((f32[1,5,8,512]{3,2,1,0:T(8,128)S(1)}, f32[1,5,8,512]{3,2,1,0:T(8,128)S(1)}, u32[]{:S(2)}, u32[]{:S(2)}) %collective-permute-start.5) | collective-permute-done | bytes 81952 | tf_op jit(solution)/shard_map/ppermute | solution.py:45
  67.2 0.0 copy-start.2
  67.2 0.0 copy-start.3
  67.2 0.0 all-to-all-done
  67.2 2.9 %fusion.1 = bf16[128,8,512]{2,1,0:T(8,128)(2,1)} fusion(f32[32,4,8,512]{3,2,1,0:T(8,128)} %all-to-all-done, f32[128]{0:T(128)S(1)} %add_multiply_fusion, f32[8,512]{1,0:T(8,128)S(1)} %get-tuple-element.12, f32[8,512]{1,0:T(8,128)S(1)} %get-tuple-element.11), kind=kLoop, calls=%fused_computation.2 | loop fusion | flops 2097152 | bytes 3179008 | tf_op jit(solution)/shard_map/convert_element_type | solution.py:73
  70.1 0.0 copy-done.2
  70.1 0.0 copy-done.3
  (10 shorter events, 0.2 us)
Async XLA Ops:
  3.8 7.5 %copy-start = (f32[4,64,2048]{2,1,0:T(8,128)S(1)}, f32[4,64,2048]{2,1,0:T(8,128)}, u32[]{:S(2)}) copy-start(f32[4,64,2048]{2,1,0:T(8,128)} %param.2) | copy-start | bytes 6291460
  3.8 63.4 %all-to-all-start = ((f32[32,4,8,512]{3,2,1,0:T(8,128)}), f32[32,4,8,512]{3,2,1,0:T(8,128)}, u32[]{:S(2)}, u32[]{:S(2)}) async-start(f32[32,4,8,512]{3,2,1,0:T(8,128)} %bitcast.44), calls=%async_computation | async-start | bytes 4194304 | tf_op jit(solution)/shard_map/all_to_all | solution.py:21
  17.3 1.9 %copy-start.1 = (f32[5,8,8,4,512]{4,2,0,3,1:T(8,128)}, f32[5,8,8,4,512]{4,2,0,3,1:T(8,128)S(1)}, u32[]{:S(2)}) copy-start(f32[5,8,8,4,512]{4,2,0,3,1:T(8,128)S(1)} %constant_dynamic-update-slice_fusion) | copy-start | bytes 7864324
  18.6 3.4 %collective-permute-start = (f32[4,4,5,8,512]{4,3,2,1,0:T(8,128)}, f32[4,4,5,8,512]{4,3,2,1,0:T(8,128)}, u32[]{:S(2)}, u32[]{:S(2)}) collective-permute-start(f32[4,4,5,8,512]{4,3,2,1,0:T(8,128)} %dynamic-slice_bitcast_fusion), channel_id=1, source_target_pairs={{0,4},{4,0},{8,12},{12,8},{16,20},{20,16},{24,28},{28,24},{1,5},{5... | collective-permute-start | bytes 3932168 | tf_op jit(solution)/shard_map/ppermute | solution.py:45
  24.1 20.3 %collective-permute-start.3 = (f32[4,5,8,512]{3,2,1,0:T(8,128)S(1)}, f32[4,5,8,512]{3,2,1,0:T(8,128)S(1)}, u32[]{:S(2)}, u32[]{:S(2)}) collective-permute-start(f32[4,5,8,512]{3,2,1,0:T(8,128)S(1)} %get-tuple-element.9), channel_id=1, source_target_pairs={{0,3},{1,2},{2,1},{3,0},{4,7},{5,6},{6,5},{7,4},{8,11},{9,10},{10,... | collective-permute-start | bytes 983048 | tf_op jit(solution)/shard_map/ppermute | solution.py:45
  26.8 22.8 %collective-permute-start.2 = (f32[4,5,8,512]{3,2,1,0:T(8,128)S(1)}, f32[4,5,8,512]{3,2,1,0:T(8,128)S(1)}, u32[]{:S(2)}, u32[]{:S(2)}) collective-permute-start(f32[4,5,8,512]{3,2,1,0:T(8,128)S(1)} %get-tuple-element.10), channel_id=1, source_target_pairs={{0,2},{1,3},{2,0},{3,1},{4,6},{5,7},{6,4},{7,5},{8,10},{9,11},{10,... | collective-permute-start | bytes 983048 | tf_op jit(solution)/shard_map/ppermute | solution.py:45
  27.3 24.1 %collective-permute-start.1 = (f32[4,5,8,512]{3,2,1,0:T(8,128)S(1)}, f32[4,5,8,512]{3,2,1,0:T(8,128)S(1)}, u32[]{:S(2)}, u32[]{:S(2)}) collective-permute-start(f32[4,5,8,512]{3,2,1,0:T(8,128)S(1)} %get-tuple-element.8), channel_id=1, source_target_pairs={{0,1},{1,0},{2,3},{3,2},{4,5},{5,4},{6,7},{7,6},{8,9},{9,8},{10,11... | collective-permute-start | bytes 983048 | tf_op jit(solution)/shard_map/ppermute | solution.py:45
  51.5 9.3 %collective-permute-start.4 = (f32[2,5,8,512]{3,2,1,0:T(8,128)S(1)}, f32[2,5,8,512]{3,2,1,0:T(8,128)S(1)}, u32[]{:S(2)}, u32[]{:S(2)}) collective-permute-start(f32[2,5,8,512]{3,2,1,0:T(8,128)S(1)} %dynamic-slice_bitcast_fusion.4), channel_id=1, source_target_pairs={{0,8},{4,12},{8,0},{12,4},{16,24},{20,28},{24,16},{28,20},{1,9},{5... | collective-permute-start | bytes 491528 | tf_op jit(solution)/shard_map/ppermute | solution.py:45
  60.9 6.2 %collective-permute-start.5 = (f32[1,5,8,512]{3,2,1,0:T(8,128)S(1)}, f32[1,5,8,512]{3,2,1,0:T(8,128)S(1)}, u32[]{:S(2)}, u32[]{:S(2)}) collective-permute-start(f32[1,5,8,512]{3,2,1,0:T(8,128)S(1)} %constant_dynamic-slice_fusion), channel_id=1, source_target_pairs={{0,16},{4,20},{8,24},{12,28},{16,0},{20,4},{24,8},{28,12},{1,17},{... | collective-permute-start | bytes 245768 | tf_op jit(solution)/shard_map/ppermute | solution.py:45
  67.2 2.9 %copy-start.2 = (f32[8,512]{1,0:T(8,128)}, f32[8,512]{1,0:T(8,128)S(1)}, u32[]{:S(2)}) copy-start(f32[8,512]{1,0:T(8,128)S(1)} %get-tuple-element.11) | copy-start | bytes 49156
  67.2 2.9 %copy-start.3 = (f32[8,512]{1,0:T(8,128)}, f32[8,512]{1,0:T(8,128)S(1)}, u32[]{:S(2)}) copy-start(f32[8,512]{1,0:T(8,128)S(1)} %get-tuple-element.12) | copy-start | bytes 49156
